TPU v7x, 512 devices: a 8x2x16 block of a 8x8x16 slice. The times are simulated.
512 devices in a mesh: groups: 2 (over y), tp: 16 (over x, core), kv: 16 (over z).
Axes of the slice: x: 8, y: 2, z: 16, core: 2. Of those that a mesh axis runs over, the one named last changes fastest.
The devices are a block of a 8x8x16 slice.
Arguments:
- prompt_rows: bfloat16 [1024, 8192], P('groups', 'kv'), parts along dimension 0, may hold values from -400 to 400
- step_rows: bfloat16 [4, 8192], P('groups', 'kv'), parts along dimension 0, may hold values from -400 to 400
- norm_gain: bfloat16 [8192], P('kv'), may hold values from 0.5 to 1.5
- w_query: bfloat16 [8192, 8192], P('kv', 'tp'), may hold values from -0.0625 to 0.0625
- w_key: bfloat16 [8192, 1024], P('kv', 'tp'), may hold values from -0.125 to 0.125
- w_value: bfloat16 [8192, 1024], P('kv', 'tp'), may hold values from -0.0625 to 0.0625
- w_output: bfloat16 [8192, 8192], P('tp', 'kv'), may hold values from -0.0625 to 0.0625
- kv_cache: bfloat16 [8, 16384, 4096], P('groups', 'kv', 'tp'), parts along dimension 0, may hold values from -250 to 250, as said below
- step_lengths: int32 [4], P('groups'), parts along dimension 0, may hold values from 4096 to 16383
- rollout_ids: int32 [4], P('groups'), parts along dimension 0, may hold values from 0 to 1, each once
- resume_offsets: int32 [4], P('groups'), parts along dimension 0, may hold values from 2048 to 15872
- stretch_rollout: int32 [1024], P('groups'), parts along dimension 0, may hold values from 0 to 1, never falling along the last dimension, each value on 1 to 384 neighbouring positions
Outputs:
- prompt_out: bfloat16 [1024, 8192], P(('groups', 'tp'), 'kv'), parts along dimension 0
- step_out: bfloat16 [4, 8192], P('groups', 'kv'), parts along dimension 0
There are 2 independent parts, one for each index of `groups`. A program takes and returns all parts, laid end to end along the dimension named above; an argument that names none is the same for every part. Nothing has to cross between parts.
Inputs may be any that keep to these rules, and one draw needn't show every extreme that they name: `kv_cache`: along the last dimension, block t of 16 holds for each j below 1 the keys then the values (128 entries each) of key-value head (t * 4) // 8 + j; blocks naming the same head are equal.
All inputs are finite; a program needn't handle non-finite values.
Results may differ from a plain program's by a relative error of at most 0.012.
The roundings to bfloat16 on the way count: a program that leaves them out, or rounds other values in their place, can miss the bound.
Values may be sent and summed in bfloat16 or wider, within the bound.
A program may use at most 64 MiB of HBM per device.

v0:
```python
import math

import jax
import jax.numpy as jnp
from jax import lax
from jax.sharding import PartitionSpec as P

D = 8192
HD = 128
SEQS = 2


EPSILON = 1e-05
THETA = 500000.0
NEGATIVE = -1e30


def swapped(block, axis, distance):
    count = lax.axis_size(axis)
    route = []
    for low in range(count):
        high = low | 1 << distance
        if high != low and high < count:
            route += [(low, high), (high, low)]
    return lax.ppermute(block, axis, route)


def split_up(value, dim, devices):
    before, after = (value.shape[:dim], value.shape[dim + 1 :])
    return jnp.moveaxis(value.reshape(*before, devices, -1, *after), dim, 0)


def sent_and_summed(value, axis, dim):
    devices = lax.axis_size(axis)
    tiles = lax.all_to_all(split_up(value, dim, devices), axis, 0, 0, tiled=True)
    return jnp.sum(tiles, axis=0)


def in_one_piece(arrays, axis, dim, along):
    widths = [math.prod(a.shape[along:]) for a in arrays]
    both = jnp.concatenate(
        [a.reshape(*a.shape[:along], w) for a, w in zip(arrays, widths)], axis=along
    )
    filled = sent_and_summed(both, axis, dim)
    tiles = jnp.split(filled, [sum(widths[:k]) for k in range(1, len(widths))], axis=along)
    return tuple(
        (b.reshape(*filled.shape[:along], *a.shape[along:]) for a, b in zip(arrays, tiles))
    )


def side_by_side(arrays, axis, dim, along):
    both = jnp.concatenate(arrays, axis=along)
    filled, at, outs = (lax.all_gather(both, axis, axis=dim, tiled=True), 0, [])
    for a in arrays:
        outs.append(lax.slice_in_dim(filled, at, at + a.shape[along], axis=along))
        at += a.shape[along]
    return tuple(outs)


def sent_to_all(value, axis):
    copies = jnp.broadcast_to(value, (lax.axis_size(axis), *value.shape))
    return lax.all_to_all(copies, axis, split_axis=0, concat_axis=0, tiled=True)


def over_copies(value, axis):
    everything = sent_to_all(value, axis)
    return jnp.max(everything, axis=0)


def packed_total(arrays, axis):
    vector, at, outs = (jnp.concatenate([a.reshape(-1) for a in arrays]), 0, [])
    total = over_copies(vector, axis)
    for a in arrays:
        outs.append(total[at : at + a.size].reshape(a.shape))
        at += a.size
    return tuple(outs)


def taken_together(value, axis):
    everything = sent_to_all(value, axis)
    return jnp.sum(everything, axis=0)


def rotate(values, positions):
    half_dim = values.shape[-1] // 2
    freq_index = jnp.arange(half_dim, dtype=jnp.float32)
    inverse = jnp.exp(freq_index * (-2.0 * math.log(THETA) / values.shape[-1]))
    angles = positions.astype(jnp.float32)[:, None] * inverse[None, :]
    cosine = jnp.cos(angles)[:, None, :]
    sine_part = jnp.sin(angles)[:, None, :]
    first_half = values[..., :half_dim]
    second_half = values[..., half_dim:]
    return jnp.concatenate(
        [
            first_half * cosine - second_half * sine_part,
            second_half * cosine + first_half * sine_part,
        ],
        axis=-1,
    )


def stretch_positions(stretch_rollout, resume_offsets):
    members = jnp.arange(resume_offsets.shape[0], dtype=jnp.int32)
    onehot = (stretch_rollout[:, None] == members[None, :]).astype(jnp.int32)
    starts = jnp.sum((stretch_rollout[:, None] < members[None, :]).astype(jnp.int32), axis=0)
    shifted = jnp.sum(onehot * (resume_offsets - starts)[None, :], axis=1)
    return shifted + jnp.arange(stretch_rollout.shape[0], dtype=jnp.int32)


def finish(query_sum, pair_sum, norm_sum, positions):
    scaling = lax.rsqrt(norm_sum / D + EPSILON)[:, None]
    row_count = query_sum.shape[0]
    key_width = pair_sum.shape[1] // 2
    queries = rotate((query_sum * scaling).reshape(row_count, -1, HD), positions).reshape(
        row_count, -1
    )
    key_rows = rotate(
        (pair_sum[:, :key_width] * scaling).reshape(row_count, -1, HD), positions
    ).reshape(row_count, -1)
    value_rows = pair_sum[:, key_width:] * scaling
    return (
        queries.astype(jnp.bfloat16),
        jnp.concatenate([key_rows, value_rows], axis=1).astype(jnp.bfloat16),
    )


def absorb(carried, scores, allowed, values, form):
    running_max, running_sum, running_out = carried
    masked = jnp.where(allowed, scores, NEGATIVE)
    new_max = jnp.maximum(running_max, jnp.max(masked, axis=-1))
    weights = jnp.where(allowed, jnp.exp(scores - new_max[..., None]), 0.0)
    factor = jnp.exp(running_max - new_max)
    new_sum = running_sum * factor + jnp.sum(weights, axis=-1)
    added = jnp.einsum(
        form, weights.astype(jnp.bfloat16), values, preferred_element_type=jnp.float32
    )
    return (new_max, new_sum, running_out * factor[..., None] + added)


def on_device(
    prompt_rows,
    step_rows,
    norm_gain,
    w_query,
    w_key,
    w_value,
    w_output,
    kv_cache,
    step_lengths,
    rollout_ids,
    resume_offsets,
    stretch_rollout,
):
    kv_index = lax.axis_index("kv")
    kv_count = lax.axis_size("kv")
    prompt_count = prompt_rows.shape[0]
    step_count = step_rows.shape[0]
    block_rows = kv_cache.shape[1]
    local_heads = kv_cache.shape[2] // (2 * HD)
    inverse_root = 1.0 / math.sqrt(HD)
    other_key, other_value = swapped((w_key, w_value), "tp", 0)
    even_side = lax.axis_index("tp") % 2 == 0
    key_weight = jnp.where(
        even_side, jnp.concatenate([w_key, other_key], 1), jnp.concatenate([other_key, w_key], 1)
    )
    value_weight = jnp.where(
        even_side,
        jnp.concatenate([w_value, other_value], 1),
        jnp.concatenate([other_value, w_value], 1),
    )
    all_rows = jnp.concatenate([prompt_rows, step_rows], axis=0)
    widened = all_rows.astype(jnp.float32)
    square_sum = jnp.sum(widened * widened, axis=1)
    normed = (widened * norm_gain.astype(jnp.float32)[None, :]).astype(jnp.bfloat16)
    query_part = jnp.dot(normed, w_query, preferred_element_type=jnp.float32)
    pair_part = jnp.dot(
        normed,
        jnp.concatenate([key_weight, value_weight], axis=1),
        preferred_element_type=jnp.float32,
    )
    positions = jnp.concatenate([stretch_positions(stretch_rollout, resume_offsets), step_lengths])
    row_total = prompt_count + step_count
    extra_rows = -row_total % kv_count
    query_padded = jnp.pad(query_part, ((0, extra_rows), (0, 0)))
    pair_padded = jnp.pad(pair_part, ((0, extra_rows), (0, 0)))
    square_padded = jnp.pad(square_sum, ((0, extra_rows),))
    position_padded = jnp.pad(positions, ((0, extra_rows),))
    query_sum, pair_sum, norm_sum = in_one_piece(
        (query_padded, pair_padded, square_padded), "kv", 0, 1
    )
    share_rows = query_sum.shape[0]
    share_positions = lax.dynamic_slice_in_dim(
        position_padded, kv_index * share_rows, share_rows, 0
    )
    query_share, pair_share = finish(query_sum, pair_sum, norm_sum, share_positions)
    queries_all, pair_all = side_by_side((query_share, pair_share), "kv", 0, 1)
    queries = queries_all[:row_total]
    pair_rows = pair_all[:row_total]
    total_rows = queries.shape[0]
    queries = queries.reshape(total_rows, local_heads, -1, HD)
    pair_rows = pair_rows.reshape(total_rows, 2, local_heads, HD)
    group_width = queries.shape[2]
    prompt_query = queries[:prompt_count]
    step_query = queries[prompt_count:]
    prompt_keys = pair_rows[:prompt_count, 0]
    prompt_values = pair_rows[:prompt_count, 1]
    step_keys = pair_rows[prompt_count:, 0]
    step_values = pair_rows[prompt_count:, 1]
    cache_blocks = kv_cache.reshape(kv_cache.shape[0], block_rows, local_heads, 2, HD)
    block_start = kv_index * block_rows
    key_positions = block_start + jnp.arange(block_rows, dtype=jnp.int32)
    stretch_index = jnp.arange(prompt_count, dtype=jnp.int32)

    def initial(row_count):
        return (
            jnp.full((row_count, local_heads, group_width), NEGATIVE, jnp.float32),
            jnp.zeros((row_count, local_heads, group_width), jnp.float32),
            jnp.zeros((row_count, local_heads, group_width, HD), jnp.float32),
        )

    prompt_state = initial(prompt_count)

    def whole_stretch(current):
        allowed = (
            (stretch_rollout[:, None] == stretch_rollout[None, :])
            & (stretch_index[None, :] <= stretch_index[:, None])
        )[:, None, None, :]
        scores = (
            jnp.einsum(
                "qjgd,pjd->qjgp", prompt_query, prompt_keys, preferred_element_type=jnp.float32
            )
            * inverse_root
        )
        return absorb(current, scores, allowed, prompt_values, "qjgp,pjd->qjgd")

    prompt_state = lax.cond(kv_index == 0, whole_stretch, lambda current: current, prompt_state)
    for member in range(resume_offsets.shape[0]):
        slot_index = SEQS + rollout_ids[member]
        slot_block = lax.dynamic_index_in_dim(cache_blocks, slot_index, 0, keepdims=False)
        limit_pos = resume_offsets[member]

        def attend(current):
            allowed = (stretch_rollout == member)[:, None, None, None] & (
                key_positions < limit_pos
            )[None, None, None, :]
            scores = (
                jnp.einsum(
                    "qjgd,pjd->qjgp",
                    prompt_query,
                    slot_block[:, :, 0, :],
                    preferred_element_type=jnp.float32,
                )
                * inverse_root
            )
            return absorb(current, scores, allowed, slot_block[:, :, 1, :], "qjgp,pjd->qjgd")

        prompt_state = lax.cond(
            block_start < limit_pos, attend, lambda current: current, prompt_state
        )
    step_cache = cache_blocks[:step_count]
    step_scores = (
        jnp.einsum(
            "sjgd,spjd->sjgp",
            step_query,
            step_cache[:, :, :, 0, :],
            preferred_element_type=jnp.float32,
        )
        * inverse_root
    )
    step_allowed = (key_positions[None, :] < step_lengths[:, None])[:, None, None, :]
    step_state = absorb(
        initial(step_count), step_scores, step_allowed, step_cache[:, :, :, 1, :], "sjgp,spjd->sjgd"
    )
    own_scores = (
        jnp.einsum("sjgd,sjd->sjg", step_query, step_keys, preferred_element_type=jnp.float32)[
            ..., None
        ]
        * inverse_root
    )
    step_state = absorb(step_state, own_scores, kv_index == 0, step_values, "sjgp,sjd->sjgd")
    prompt_top, step_top = packed_total((prompt_state[0], step_state[0]), "kv")
    prompt_factor = jnp.exp(prompt_state[0] - prompt_top)
    step_factor = jnp.exp(step_state[0] - step_top)
    prompt_sum, prompt_mixed, step_sum, step_mixed = lax.psum(
        (
            prompt_state[1] * prompt_factor,
            prompt_state[2] * prompt_factor[..., None],
            step_state[1] * step_factor,
            step_state[2] * step_factor[..., None],
        ),
        "kv",
    )
    prompt_mix = (
        (prompt_mixed / prompt_sum[..., None]).astype(jnp.bfloat16).reshape(prompt_count, -1)
    )
    step_mix = (step_mixed / step_sum[..., None]).astype(jnp.bfloat16).reshape(step_count, -1)
    projected = jnp.dot(
        jnp.concatenate([prompt_mix, step_mix], axis=0),
        w_output,
        preferred_element_type=jnp.float32,
    )
    prompt_part = sent_and_summed(projected[:prompt_count], "tp", 0)
    step_part = taken_together(projected[prompt_count:], "tp")
    return (prompt_part.astype(jnp.bfloat16), step_part.astype(jnp.bfloat16))


def solution(mesh):
    in_specs = (
        P("groups", "kv"),
        P("groups", "kv"),
        P("kv"),
        P("kv", "tp"),
        P("kv", "tp"),
        P("kv", "tp"),
        P("tp", "kv"),
        P("groups", "kv", "tp"),
        P("groups"),
        P("groups"),
        P("groups"),
        P("groups"),
    )
    out_specs = (P(("groups", "tp"), "kv"), P("groups", "kv"))
    return jax.shard_map(
        on_device, mesh=mesh, in_specs=in_specs, out_specs=out_specs, check_vma=False
    )
```

profile of v0, /device:TPU:65, one launch (start us, length us, event | category | flops | bytes accessed | tf_op | source)
XLA Modules:
  0.0 455.8 jit_solution(1848168938536869961)
XLA Ops:
  7.2 43.5 %collective-permute-start = (bf16[512,64]{0,1:T(8,128)(2,1)}, bf16[512,64]{0,1:T(8,128)(2,1)S(1)}, u32[]{:S(2)}, u32[]{:S(2)}) collective-permute-start(bf16[512,64]{0,1:T(8,128)(2,1)} %param.22), channel_id=1, source_target_pairs={{0,16},{16,0},{32,48},{48,32},{64,80},{80,64},{96,112},{112,96},{1... | collective-permute-start | bytes 196616 | tf_op jit(solution)/shard_map/ppermute | solution.py:25
  50.7 2.0 collective-permute-start.1
  53.4 1.5 fusion.81
  56.7 1.4 fusion.79
  58.3 1.5 pad_maximum_fusion
  59.8 4.8 %all-to-all-start = ((f32[16,33,769]{2,1,0:T(8,128)}), f32[16,33,769]{2,1,0:T(8,128)}, u32[]{:S(2)}, u32[]{:S(2)}) async-start(f32[16,33,769]{2,1,0:T(8,128)} %pad_maximum_fusion), calls=%async_computation | async-start | bytes 4587520 | tf_op jit(solution)/shard_map/all_to_all | solution.py:35
  69.1 3.0 copy.132
  74.7 89.8 %all-to-all-done = f32[16,33,769]{2,1,0:T(8,128)} async-done(((f32[16,33,769]{2,1,0:T(8,128)}), f32[16,33,769]{2,1,0:T(8,128)}, u32[]{:S(2)}, u32[]{:S(2)}) %all-to-all-start) | async-done | bytes 1624160 | tf_op jit(solution)/shard_map/all_to_all | solution.py:35
  164.6 1.8 reduce_sum.105
  167.2 31.0 %all-gather = bf16[16,33,768]{2,1,0:T(8,128)(2,1)} all-gather(bf16[1,33,768]{2,1,0:T(8,128)(2,1)S(1)} %maximum_bitcast_fusion), channel_id=1, replica_groups=mesh['groups'=2,'tp'=16,'kv'=16] {'kv'}, dimensions={0}, use_global_device_ids=true | all-gather | bytes 861696 | tf_op jit(solution)/shard_map/all_gather | solution.py:53
  198.2 1.5 reshape.623
  200.8 3.6 conditional.3
  202.9 1.5 fusion.15
  204.4 8.5 %conditional.4 = (f32[512,1,4]{0,2,1:T(4,128)S(1)}, f32[512,1,4]{0,2,1:T(4,128)S(1)}, f32[512,1,4,128]{3,0,2,1:T(8,128)S(1)}, f32[512,1,4,128]{0,3,2,1:T(8,128)S(1)}) conditional(s32[]{:T(128)} %convert_element_type.68, (f32[512,1,4]{0,2,1:T(4,128)S(1)}, f32[512,1,4]{0,2,1:T(4,128)S(1)}, f32[512,1,4,128]{3,0,2,1:T(8,128)S(1)}) %conditional.3, ...), branch_computations={%region_8.9_spmd, %region_9.12_spmd} | conditional | flops 1097866752 | bytes 34743360 | solution.py:257
  205.6 2.6 fusion.25
  208.2 2.5 fusion.37
  210.7 1.8 fusion.29
  212.9 13.4 %conditional.5 = ((f32[512,1,4]{0,2,1:T(4,128)S(1)}, f32[512,1,4]{0,2,1:T(4,128)S(1)}, f32[512,1,4,128]{0,3,2,1:T(8,128)S(1)})) conditional(s32[]{:T(128)} %convert_element_type.67, (f32[512,1,4]{0,2,1:T(4,128)S(1)}, f32[512,1,4]{0,2,1:T(4,128)S(1)}, f32[512,1,4,128]{0,3,2,1:T(8,128)S(1)}) %tuple.67, (s32[512]{0:T(512)S(1)}, s32[]{:T(128)}, ...), branch_computations={%region_12.13_spmd, %region_13.16_spmd.clone} | conditional | flops 1097866752 | bytes 42083432 | solution.py:257
  215.8 4.0 copy.136
  220.9 1.6 fusion.49
  222.5 2.0 fusion.61
  224.5 1.8 fusion.53
  228.8 4.0 all-to-all-start.1
  233.9 10.4 %all-to-all-done.1 = f32[16,1,2056]{2,1,0:T(1,128)S(1)} async-done(((f32[16,1,2056]{2,1,0:T(1,128)}), f32[16,1,2056]{2,1,0:T(1,128)S(1)}, u32[]{:S(2)}, u32[]{:S(2)}) %all-to-all-start.1) | async-done | bytes 131616 | tf_op jit(solution)/shard_map/all_to_all | solution.py:62
  245.4 1.8 fusion.86
  250.1 46.8 %all-reduce.4 = (f32[2,1,4,128]{3,2,0,1:T(4,128)S(1)}, f32[2,4]{1,0:T(2,128)S(1)}, f32[512,4]{1,0:T(8,128)S(1)}) all-reduce(f32[2,1,4,128]{3,2,0,1:T(4,128)S(1)} %fusion.72, f32[2,4]{1,0:T(2,128)S(1)} %get-tuple-element.329, f32[512,4]{1,0:T(8,128)S(1)} %get-tuple-element.342), channel_id=1, replica_groups=mesh['groups'=2,'tp'=16,'kv'=16] {'kv'}, use_global_device_ids=true, to_apply=%region_20.21 | all-reduce | flops 3080 | bytes 24640 | tf_op jit(solution)/shard_map/psum | solution.py:284
  297.2 90.8 %all-reduce.7.cloned.1.call-done = f32[512,1,4,128]{0,3,2,1:T(8,128)} async-done(((f32[512,1,4,128]{0,3,2,1:T(8,128)}), f32[512,1,4,128]{0,3,2,1:T(8,128)}) %all-reduce.7.cloned.1.call-update) | async-done | bytes 1048592 | tf_op jit(solution)/shard_map/psum | solution.py:284
  389.4 1.5 fusion.75
  391.6 17.2 %all-to-all-start.3 = ((f32[16,2,512]{2,1,0:T(2,128)}), f32[16,2,512]{2,1,0:T(2,128)S(1)}, u32[]{:S(2)}, u32[]{:S(2)}) async-start(f32[16,2,512]{2,1,0:T(2,128)} %broadcast_in_dim.147), calls=%async_computation.3 | async-start | bytes 131072 | tf_op jit(solution)/shard_map/all_to_all | solution.py:62
  409.8 6.7 %all-to-all-done.3 = f32[16,2,512]{2,1,0:T(2,128)S(1)} async-done(((f32[16,2,512]{2,1,0:T(2,128)}), f32[16,2,512]{2,1,0:T(2,128)S(1)}, u32[]{:S(2)}, u32[]{:S(2)}) %all-to-all-start.3) | async-done | bytes 65568 | tf_op jit(solution)/shard_map/all_to_all | solution.py:62
  416.5 3.8 all-to-all-start.2
  421.0 27.3 %all-to-all-done.2 = f32[16,32,512]{2,1,0:T(8,128)S(1)} async-done(((f32[16,32,512]{2,1,0:T(8,128)}), f32[16,32,512]{2,1,0:T(8,128)S(1)}, u32[]{:S(2)}, u32[]{:S(2)}) %all-to-all-start.2) | async-done | bytes 1048608 | tf_op jit(solution)/shard_map/all_to_all | solution.py:35
  (122 shorter events, 27.3 us)
Async XLA Ops:
  7.2 46.2 %copy-start = (bf16[512,512]{1,0:T(8,128)(2,1)S(1)}, bf16[512,512]{1,0:T(8,128)(2,1)}, u32[]{:S(2)}) copy-start(bf16[512,512]{1,0:T(8,128)(2,1)} %param.21) | copy-start | bytes 1572868
  7.2 49.4 %copy-start.6 = (bf16[512,64]{0,1:T(8,128)(2,1)S(1)}, bf16[512,64]{0,1:T(8,128)(2,1)}, u32[]{:S(2)}) copy-start(bf16[512,64]{0,1:T(8,128)(2,1)} %param.22) | copy-start | bytes 196612
  7.2 49.5 %copy-start.7 = (bf16[512,64]{0,1:T(8,128)(2,1)S(1)}, bf16[512,64]{0,1:T(8,128)(2,1)}, u32[]{:S(2)}) copy-start(bf16[512,64]{0,1:T(8,128)(2,1)} %param.23) | copy-start | bytes 196612
  7.2 49.5 %copy-start.8 = (bf16[2,512]{1,0:T(2,128)(2,1)S(1)}, bf16[2,512]{1,0:T(2,128)(2,1)}, u32[]{:S(2)}) copy-start(bf16[2,512]{1,0:T(2,128)(2,1)} %param.19) | copy-start | bytes 6148
  7.2 49.4 %collective-permute-start = (bf16[512,64]{0,1:T(8,128)(2,1)}, bf16[512,64]{0,1:T(8,128)(2,1)S(1)}, u32[]{:S(2)}, u32[]{:S(2)}) collective-permute-start(bf16[512,64]{0,1:T(8,128)(2,1)} %param.22), channel_id=1, source_target_pairs={{0,16},{16,0},{32,48},{48,32},{64,80},{80,64},{96,112},{112,96},{1... | collective-permute-start | bytes 196616 | tf_op jit(solution)/shard_map/ppermute | solution.py:25
  50.7 5.9 %collective-permute-start.1 = (bf16[512,64]{0,1:T(8,128)(2,1)}, bf16[512,64]{0,1:T(8,128)(2,1)S(1)}, u32[]{:S(2)}, u32[]{:S(2)}) collective-permute-start(bf16[512,64]{0,1:T(8,128)(2,1)} %param.23), channel_id=1, source_target_pairs={{0,16},{16,0},{32,48},{48,32},{64,80},{80,64},{96,112},{112,96},{1... | collective-permute-start | bytes 196616 | tf_op jit(solution)/shard_map/ppermute | solution.py:25
  58.2 6.4 %copy-start.9 = (s32[2]{0:T(128)S(1)}, s32[2]{0:T(128)}, u32[]{:S(2)}) copy-start(s32[2]{0:T(128)} %param.27) | copy-start | bytes 28
  58.3 8.8 %copy-start.5 = (s32[512]{0:T(512)S(1)}, s32[512]{0:T(512)}, u32[]{:S(2)}) copy-start(s32[512]{0:T(512)} %param.29) | copy-start | bytes 6148
  58.3 8.9 %copy-start.10 = (s32[2]{0:T(128)S(1)}, s32[2]{0:T(128)}, u32[]{:S(2)}) copy-start(s32[2]{0:T(128)} %param.28) | copy-start | bytes 28
  59.8 104.8 %all-to-all-start = ((f32[16,33,769]{2,1,0:T(8,128)}), f32[16,33,769]{2,1,0:T(8,128)}, u32[]{:S(2)}, u32[]{:S(2)}) async-start(f32[16,33,769]{2,1,0:T(8,128)} %pad_maximum_fusion), calls=%async_computation | async-start | bytes 4587520 | tf_op jit(solution)/shard_map/all_to_all | solution.py:35
  69.1 5.3 %copy-start.11 = (s32[2]{0:T(128)S(1)}, s32[2]{0:T(128)}, u32[]{:S(2)}) copy-start(s32[2]{0:T(128)} %param.26) | copy-start | bytes 28
  72.1 126.1 %copy-start.1 = (bf16[4,1024,256]{1,2,0:T(8,128)(2,1)}, bf16[4,1024,256]{1,2,0:T(8,128)(2,1)S(1)}, u32[]{:S(2)}) copy-start(bf16[4,1024,256]{1,2,0:T(8,128)(2,1)S(1)} %copy.132) | copy-start | bytes 6291460
  205.6 2.6 copy-start.3
  220.9 1.6 copy-start.4
  226.4 23.4 %copy-start.2 = (bf16[2,1024,256]{1,2,0:T(8,128)(2,1)S(1)}, bf16[2,1024,256]{1,2,0:T(8,128)(2,1)}, u32[]{:S(2)}) copy-start(bf16[2,1024,256]{1,2,0:T(8,128)(2,1)} %slice.160) | copy-start | bytes 3145732
  228.8 15.5 %all-to-all-start.1 = ((f32[16,1,2056]{2,1,0:T(1,128)}), f32[16,1,2056]{2,1,0:T(1,128)S(1)}, u32[]{:S(2)}, u32[]{:S(2)}) async-start(f32[16,1,2056]{2,1,0:T(1,128)} %broadcast_in_dim.144), calls=%async_computation.1 | async-start | bytes 278528 | tf_op jit(solution)/shard_map/all_to_all | solution.py:62
  232.8 155.2 %all-reduce.7.cloned.1.call-start = ((), (), s32[]{:S(2)}) async-start(), calls=%async_computation.4 | async-start | bytes 2097152 | tf_op jit(solution)/shard_map/psum | solution.py:284
  391.6 25.0 %all-to-all-start.3 = ((f32[16,2,512]{2,1,0:T(2,128)}), f32[16,2,512]{2,1,0:T(2,128)S(1)}, u32[]{:S(2)}, u32[]{:S(2)}) async-start(f32[16,2,512]{2,1,0:T(2,128)} %broadcast_in_dim.147), calls=%async_computation.3 | async-start | bytes 131072 | tf_op jit(solution)/shard_map/all_to_all | solution.py:62
  416.5 31.7 %all-to-all-start.2 = ((f32[16,32,512]{2,1,0:T(8,128)}), f32[16,32,512]{2,1,0:T(8,128)S(1)}, u32[]{:S(2)}, u32[]{:S(2)}) async-start(f32[16,32,512]{2,1,0:T(8,128)} %bitcast.53), calls=%async_computation.2 | async-start | bytes 2097152 | tf_op jit(solution)/shard_map/all_to_all | solution.py:35
Sparse Core Ops, SparseCore 0:
  249.6 138.3 all-reduce.6
where the time goes:
time: 457 us; the launch traced here: 456 us
  waiting for transfers between devices  225 us (49%)
  blocking collectives  77.8 us (17%)
  starting transfers between devices  75.5 us (17%)
  local copies, waits for them, and re-layouts  22.2 us (5%)
  other arithmetic  19.4 us (4%)
  between operations  17.7 us (4%)
  matrix products  17.1 us (4%)
    all_to_all x2, waiting for transfers between devices, sent_and_summed(): lax.all_to_all(split_up(value, dim, devices), axis, 0, 0, tiled=True)  117 us
    psum x1, waiting for transfers between devices, on_device(): lax.psum((prompt_state[1] * prompt_factor, prompt_state[2] * prompt_facto...  90.8 us
    psum x1, blocking collectives, on_device(): lax.psum((prompt_state[1] * prompt_factor, prompt_state[2] * prompt_facto...  46.8 us
    ppermute x2, starting transfers between devices, swapped(): return lax.ppermute(block, axis, route)  45.5 us
    all_gather x1, blocking collectives, side_by_side(): filled, at, outs = (lax.all_gather(both, axis, axis=dim, tiled=True), 0, [])  31 us
    all_to_all x2, starting transfers between devices, sent_to_all(): return lax.all_to_all(copies, axis, split_axis=0, concat_axis=0, tiled=True)  21.2 us
    all_to_all x2, waiting for transfers between devices, sent_to_all(): return lax.all_to_all(copies, axis, split_axis=0, concat_axis=0, tiled=True)  17.1 us
  transfers between devices with their start and end apart: 7, of which 5 were waited for; matrix products, arithmetic and copies ran while one was open for 3% of the time, Pallas kernels for 0%

commit v1 on v0

v1 whole, which is shorter than its diff:
```python
import functools
import math

import jax
import jax.numpy as jnp
import numpy as np
from jax import lax
from jax.experimental import pallas as pl
from jax.experimental.pallas import tpu as pltpu
from jax.sharding import PartitionSpec as P

HD = 128
SEQS = 2
EPSILON = 1e-05
THETA = 500000.0
NEGATIVE = -1e30
EXPONENT = math.log2(math.e) / math.sqrt(HD)
F32, BF16 = jnp.float32, jnp.bfloat16
MESH = pl.DeviceIdType.MESH


def iota(shape, dim):
    return lax.broadcasted_iota(jnp.int32, shape, dim)


def dot(a, b):
    return jnp.dot(a, b, preferred_element_type=F32)


def dot_t(a, b):
    return lax.dot_general(a, b, (((1,), (1,)), ((), ())), preferred_element_type=F32)


def far_first(me, count, j):
    distance = count // 2 - (j + 1) // 2
    return lax.rem(me + distance * (2 * lax.rem(j, 2) - 1) + count, count)


def high_low(value):
    high = value.astype(BF16).astype(F32)
    return high, value - high


def rotated(value, cosine, sine):
    return value * cosine + pltpu.roll(value, HD // 2, 1) * sine


def angles(position, inverse):
    angle = position * inverse
    lane = iota(angle.shape, 1)
    sine = jnp.sin(angle)
    return jnp.cos(angle), jnp.where(lane < HD // 2, -sine, sine)


def stacked(rows):
    return jnp.concatenate([rows[:, at : at + HD] for at in range(0, rows.shape[1], HD)], axis=0)


def attend(queries, second, allowed, keys, values):
    both = jnp.concatenate(
        [jnp.where(second, 0.0, queries), jnp.where(second, queries, 0.0)], axis=1
    ).astype(BF16)
    scores = jnp.where(allowed, dot_t(both, keys), NEGATIVE)
    top = jnp.max(scores, axis=1, keepdims=True)
    weights = jnp.exp2((scores - top) * EXPONENT)
    total = jnp.sum(weights, axis=1, keepdims=True)
    mixed = dot(weights.astype(BF16), values)
    mixed = jnp.where(second, mixed[:, HD:], mixed[:, :HD])
    some = top > 0.1 * NEGATIVE
    return jnp.where(some, mixed, 0.0), top, jnp.where(some, total, 0.0)


def packed(mixed, top, total, rows):
    heads = mixed.shape[0] // rows
    lane = iota((rows, HD), 1)
    tile = jnp.zeros((rows, HD), F32)
    high, rest = high_low(top)
    middle, low = high_low(rest)
    total_high, total_low = high_low(total)
    for k, column in enumerate((high, middle, low, total_high, total_low)):
        for h in range(heads):
            tile = jnp.where(lane == k * heads + h, column[h * rows : (h + 1) * rows], tile)
    return jnp.concatenate(
        [mixed[h * rows : (h + 1) * rows] for h in range(heads)] + [tile], axis=1
    ).astype(BF16)


def combined(parts_ref, count):
    width = parts_ref.shape[2] - HD
    heads = width // HD
    tops, totals = [], []
    for s in range(count):
        tile = parts_ref[s, :, width:].astype(F32)
        shift = lambda k: pltpu.roll(tile, HD - k * heads, 1)
        tops.append(tile + shift(1) + shift(2))
        totals.append(shift(3) + shift(4))
    top = functools.reduce(jnp.maximum, tops)
    weights = [jnp.exp2((t - top) * EXPONENT) for t in tops]
    total = functools.reduce(jnp.add, [w * t for w, t in zip(weights, totals)])
    outs = []
    for h in range(heads):
        mixed = 0.0
        for s in range(count):
            mixed += weights[s][:, h : h + 1] * parts_ref[s, :, h * HD : (h + 1) * HD].astype(F32)
        outs.append(mixed / total[:, h : h + 1])
    return jnp.concatenate(outs, axis=1)


def kernel(
    kv_count,
    tp_count,
    rows_ref,
    step_ref,
    gain_ref,
    wq_ref,
    wk_ref,
    wv_ref,
    wo_hbm,
    cache_hbm,
    lengths_ref,
    ids_ref,
    offsets_ref,
    rollout_ref,
    inverse_ref,
    out_ref,
    step_out_ref,
    wo_ref,
    cache_ref,
    a_send,
    a_recv,
    aux_recv,
    pair_send,
    pair_recv,
    q_recv,
    c_send,
    c_recv,
    cs_recv,
    m_recv,
    e_send,
    e_recv,
    es_recv,
    keys_ref,
    values_ref,
    step_keys_ref,
    step_values_ref,
    local_sem,
    pair_sem,
    send_sem,
    recv_sem,
):
    me = lax.axis_index("kv")
    tp = lax.axis_index("tp")
    features = rows_ref.shape[1]
    row_count = rows_ref.shape[0]
    width = wq_ref.shape[1]
    heads = width // HD
    share = row_count // kv_count
    block = cache_ref.shape[1]
    total_features = features * kv_count
    partner = tp + 1 - 2 * lax.rem(tp, 2)

    wo_copy = pltpu.make_async_copy(wo_hbm, wo_ref, local_sem.at[0])
    cache_copy = pltpu.make_async_copy(cache_hbm, cache_ref, local_sem.at[1])
    wo_copy.start()
    cache_copy.start()

    barrier = pltpu.get_barrier_semaphore()

    def greet(axis, count, here):
        def one(j, carry):
            pl.semaphore_signal(
                barrier,
                inc=1,
                device_id={axis: far_first(here, count, j)},
                device_id_type=MESH,
            )
            return carry

        lax.fori_loop(0, count - 1, one, 0)

    greet("kv", kv_count, me)
    greet("tp", tp_count, tp)

    def remote(phase, axis, peer, source, slot_ref, slot):
        return pltpu.make_async_remote_copy(
            src_ref=source,
            dst_ref=slot_ref.at[slot],
            send_sem=send_sem.at[phase, peer],
            recv_sem=recv_sem.at[phase, slot],
            device_id={axis: peer},
            device_id_type=MESH,
        )

    def to_all(phase, axis, count, here, source, slot_ref):
        def one(j, carry):
            peer = far_first(here, count, j)
            remote(phase, axis, peer, source(peer), slot_ref, here).start()
            return carry

        lax.fori_loop(0, count - 1, one, 0)

    def arrive(phase, axis, peer, slot_ref):
        remote(phase, axis, peer, slot_ref.at[peer], slot_ref, peer).wait_recv()

    def all_arrive(phase, axis, count, here, slot_ref):
        def one(j, carry):
            arrive(phase, axis, far_first(here, count, j), slot_ref)
            return carry

        lax.fori_loop(0, count - 1, one, 0)

    def all_sent(phase, axis, count, here, source, slot_ref):
        def one(j, carry):
            peer = far_first(here, count, j)
            remote(phase, axis, peer, source(peer), slot_ref, here).wait_send()
            return carry

        lax.fori_loop(0, count - 1, one, 0)

    gain = gain_ref[...].astype(F32)
    wide = rows_ref[...].astype(F32)
    normed = (wide * gain).astype(BF16)
    step_wide = jnp.concatenate(
        [step_ref[...].astype(F32), jnp.zeros((HD - SEQS, features), F32)], axis=0
    )
    step_normed = (step_wide[:16] * gain).astype(BF16)
    ones = jnp.ones((8, features), BF16)

    def squares(value):
        high, low = high_low(value * value)
        return dot_t(ones, high.astype(BF16)) + dot_t(ones, low.astype(BF16))

    weight_pair = jnp.concatenate([wk_ref[...], wv_ref[...]], axis=1)
    square_high, square_low = high_low(
        jnp.concatenate([squares(wide), squares(step_wide)], axis=1)
    )
    step_part = jnp.concatenate(
        [dot(step_normed, wq_ref[...])[:8], dot(step_normed, weight_pair)[:8]], axis=1
    )
    aux_row = iota(step_part.shape, 0)
    aux = jnp.where(
        aux_row == SEQS, square_high, jnp.where(aux_row == SEQS + 1, square_low, step_part)
    )
    aux_recv[me] = aux.astype(BF16)
    a_send[:, :, :width] = dot(normed, wq_ref[...]).astype(BF16).reshape(kv_count, share, width)
    a_send[:, :, width:] = dot(normed, weight_pair).astype(BF16).reshape(kv_count, share, HD)
    a_recv[me] = a_send[me]

    pl.semaphore_wait(barrier, kv_count + tp_count - 2)
    aux_source = lambda peer: aux_recv.at[me]
    a_source = lambda peer: a_send.at[peer]
    to_all(0, "kv", kv_count, me, aux_source, aux_recv)
    to_all(1, "kv", kv_count, me, a_source, a_recv)

    cache_copy.wait()
    keys_ref[:block, :HD] = cache_ref[SEQS + ids_ref[0], :, :HD]
    keys_ref[:block, HD:] = cache_ref[SEQS + ids_ref[1], :, :HD]
    values_ref[:block, :HD] = cache_ref[SEQS + ids_ref[0], :, HD:]
    values_ref[:block, HD:] = cache_ref[SEQS + ids_ref[1], :, HD:]
    step_keys_ref[:block, :HD] = cache_ref[0, :, :HD]
    step_keys_ref[:block, HD:] = cache_ref[1, :, :HD]
    step_values_ref[:block, :HD] = cache_ref[0, :, HD:]
    step_values_ref[:block, HD:] = cache_ref[1, :, HD:]
    wo_copy.wait()

    first_count = jnp.sum(
        jnp.sum((rollout_ref[...] == 0).astype(F32), axis=1, keepdims=True), axis=0, keepdims=True
    )
    offset_0 = offsets_ref[0].astype(F32)
    offset_1 = offsets_ref[1].astype(F32)
    own_row = (iota((share, 1), 0) + me * share).astype(F32)
    position = jnp.where(own_row >= first_count, own_row + offset_1 - first_count, own_row + offset_0)
    step_row = iota((8, 1), 0)
    step_position = jnp.where(step_row == 0, lengths_ref[0], lengths_ref[1]).astype(F32)
    inverse = inverse_ref[...]
    cosine, sine = angles(position, inverse)
    step_cosine, step_sine = angles(step_position, inverse)

    all_arrive(0, "kv", kv_count, me, aux_recv)
    aux_sum = aux_recv[0].astype(F32)
    for s in range(1, kv_count):
        aux_sum += aux_recv[s].astype(F32)
    square_row = aux_sum[SEQS : SEQS + 1] + aux_sum[SEQS + 1 : SEQS + 2]

    def own_scale(start, rows):
        shape = (rows, square_row.shape[1])
        mine = iota(shape, 1) == start + iota(shape, 0)
        squared = jnp.sum(jnp.where(mine, square_row, 0.0), axis=1, keepdims=True)
        return lax.rsqrt(squared / total_features + EPSILON)

    scale = own_scale(me * share, share)
    step_scale = own_scale(row_count, 8)
    step_raw = aux_sum * step_scale

    all_arrive(1, "kv", kv_count, me, a_recv)
    raw = a_recv[0].astype(F32)
    for s in range(1, kv_count):
        raw += a_recv[s].astype(F32)
    raw = raw * scale

    pair = jnp.concatenate([raw[:, width:], step_raw[:, width:]], axis=0)
    pair_send[...] = pair
    pair_copy = pltpu.make_async_remote_copy(
        src_ref=pair_send,
        dst_ref=pair_recv,
        send_sem=pair_sem.at[0],
        recv_sem=pair_sem.at[1],
        device_id={"tp": partner},
        device_id_type=MESH,
    )
    pair_copy.start()
    q_recv[me] = jnp.concatenate(
        [rotated(raw[:, at : at + HD], cosine, sine) for at in range(0, width, HD)], axis=1
    ).astype(BF16)
    q_source = lambda peer: q_recv.at[me]
    to_all(2, "kv", kv_count, me, q_source, q_recv)

    step_queries = jnp.concatenate(
        [rotated(step_raw[:, at : at + HD], step_cosine, step_sine) for at in range(0, width, HD)],
        axis=0,
    )

    pair_copy.wait()
    other = pair_recv[...]
    lane = iota(other.shape, 1)
    even = iota(other.shape, 0) * 0 + lax.rem(tp, 2) == 0
    left = jnp.where(even, pair, other)
    right = jnp.where(even, other, pair)
    key_raw = jnp.where(lane < HD // 2, left, pltpu.roll(right, HD // 2, 1))
    value_rows = jnp.where(lane < HD // 2, pltpu.roll(left, HD // 2, 1), right)
    own_keys = rotated(key_raw[:share], cosine, sine)
    step_keys = rotated(key_raw[share:], step_cosine, step_sine)

    def tail(rows):
        filled = jnp.concatenate([rows, jnp.zeros((HD - rows.shape[0], HD), F32)], axis=0)
        return jnp.concatenate([filled, filled], axis=1).astype(BF16)

    keys_ref[block:, :] = tail(own_keys)
    values_ref[block:, :] = tail(value_rows[:share])
    step_keys_ref[block:, :] = tail(step_keys)
    step_values_ref[block:, :] = tail(value_rows[share:])

    key_count = block + HD
    key_lane = iota((1, key_count), 1)
    key_position = key_lane + me * block
    stack_row = iota((heads * 8, 1), 0)
    sequence = lax.rem(stack_row, 8)
    step_limit = jnp.where(sequence == 0, lengths_ref[0], lengths_ref[1])
    own_lane = jnp.where(key_lane * 0 + me == 0, key_lane - block, -1)
    step_allowed = ((key_lane < block) & (key_position < step_limit)) | (own_lane == sequence)
    step_mixed = attend(
        step_queries, sequence > 0, step_allowed, step_keys_ref[...], step_values_ref[...]
    )
    cs_recv[me] = packed(*step_mixed, 8)
    cs_source = lambda peer: cs_recv.at[me]
    to_all(3, "kv", kv_count, me, cs_source, cs_recv)

    row_in_chunk = lax.rem(iota((heads * share, 1), 0), share)

    def one_chunk(j, carry):
        owner = jnp.where(j == 0, me, far_first(me, kv_count, j - 1))

        @pl.when(j > 0)
        def _():
            arrive(2, "kv", owner, q_recv)

        row = row_in_chunk + owner * share
        second = row.astype(F32) >= first_count
        limit = jnp.where(second, offsets_ref[1], offsets_ref[0])
        tail_key = key_lane[:, block:] - block + me * share
        tail_second = tail_key.astype(F32) >= first_count
        allowed = jnp.concatenate(
            [
                (key_position[:, :block] < limit).astype(F32),
                jnp.where(
                    (tail_key <= row)
                    & (tail_key < (me + 1) * share)
                    & (tail_second.astype(F32) == second.astype(F32)),
                    1.0,
                    0.0,
                ),
            ],
            axis=1,
        )
        queries = stacked(q_recv[owner].astype(F32))
        mixed = attend(queries, second, allowed > 0.5, keys_ref[...], values_ref[...])
        message = packed(*mixed, share)

        @pl.when(j == 0)
        def _():
            c_recv[me] = message

        @pl.when(j > 0)
        def _():
            c_send[owner] = message
            remote(4, "kv", owner, c_send.at[owner], c_recv, me).start()

        return carry

    lax.fori_loop(0, kv_count, one_chunk, 0)

    all_arrive(3, "kv", kv_count, me, cs_recv)
    step_mix = combined(cs_recv, kv_count)
    step_mix = jnp.concatenate([step_mix, jnp.zeros_like(step_mix)], axis=0).astype(BF16)
    es_recv[tp] = dot(step_mix, wo_ref[...])[:8].astype(BF16)
    es_source = lambda peer: es_recv.at[tp]
    to_all(5, "tp", tp_count, tp, es_source, es_recv)

    all_arrive(4, "kv", kv_count, me, c_recv)
    m_recv[me] = combined(c_recv, kv_count).astype(BF16)
    m_source = lambda peer: m_recv.at[me]
    to_all(6, "kv", kv_count, me, m_source, m_recv)

    def one_product(j, carry):
        owner = jnp.where(j == 0, me, far_first(me, kv_count, j - 1))

        @pl.when(j > 0)
        def _():
            arrive(6, "kv", owner, m_recv)

        product = dot(m_recv[owner], wo_ref[...]).astype(BF16)

        @pl.when(owner == tp)
        def _():
            e_recv[tp] = product

        @pl.when(owner != tp)
        def _():
            e_send[owner] = product
            remote(7, "tp", owner, e_send.at[owner], e_recv, tp).start()

        return carry

    lax.fori_loop(0, kv_count, one_product, 0)

    all_arrive(5, "tp", tp_count, tp, es_recv)
    step_total = es_recv[0].astype(F32)
    for s in range(1, tp_count):
        step_total += es_recv[s].astype(F32)
    step_out_ref[...] = step_total[:SEQS].astype(BF16)
    all_arrive(7, "tp", tp_count, tp, e_recv)
    total = e_recv[0].astype(F32)
    for s in range(1, tp_count):
        total += e_recv[s].astype(F32)
    out_ref[...] = total.astype(BF16)

    all_sent(0, "kv", kv_count, me, aux_source, aux_recv)
    all_sent(1, "kv", kv_count, me, a_source, a_recv)
    all_sent(2, "kv", kv_count, me, q_source, q_recv)
    all_sent(3, "kv", kv_count, me, cs_source, cs_recv)
    all_sent(4, "kv", kv_count, me, lambda peer: c_send.at[peer], c_recv)
    all_sent(5, "tp", tp_count, tp, es_source, es_recv)
    all_sent(6, "kv", kv_count, me, m_source, m_recv)
    all_sent(7, "tp", tp_count, tp, lambda peer: e_send.at[peer], e_recv)


def on_device(
    prompt_rows,
    step_rows,
    norm_gain,
    w_query,
    w_key,
    w_value,
    w_output,
    kv_cache,
    step_lengths,
    rollout_ids,
    resume_offsets,
    stretch_rollout,
):
    kv_count = lax.axis_size("kv")
    tp_count = lax.axis_size("tp")
    row_count, features = prompt_rows.shape
    width = w_query.shape[1]
    out_width = w_output.shape[1]
    share = row_count // kv_count
    key_count = kv_cache.shape[1] + HD
    frequency = np.exp(np.arange(HD // 2) * (-2.0 * math.log(THETA) / HD)).astype(np.float32)
    inverse = jnp.asarray(np.concatenate([frequency, frequency])[None, :])
    vmem = pl.BlockSpec(memory_space=pltpu.VMEM)
    smem = pl.BlockSpec(memory_space=pltpu.SMEM)
    anywhere = pl.BlockSpec(memory_space=pl.ANY)
    scratch = [
        pltpu.VMEM(w_output.shape, BF16),
        pltpu.VMEM(kv_cache.shape, BF16),
        pltpu.VMEM((kv_count, share, width + HD), BF16),
        pltpu.VMEM((kv_count, share, width + HD), BF16),
        pltpu.VMEM((kv_count, 8, width + HD), BF16),
        pltpu.VMEM((share + 8, HD), F32),
        pltpu.VMEM((share + 8, HD), F32),
        pltpu.VMEM((kv_count, share, width), BF16),
        pltpu.VMEM((kv_count, share, width + HD), BF16),
        pltpu.VMEM((kv_count, share, width + HD), BF16),
        pltpu.VMEM((kv_count, 8, width + HD), BF16),
        pltpu.VMEM((kv_count, share, width), BF16),
        pltpu.VMEM((tp_count, share, out_width), BF16),
        pltpu.VMEM((tp_count, share, out_width), BF16),
        pltpu.VMEM((tp_count, 8, out_width), BF16),
        pltpu.VMEM((key_count, 2 * HD), BF16),
        pltpu.VMEM((key_count, 2 * HD), BF16),
        pltpu.VMEM((key_count, 2 * HD), BF16),
        pltpu.VMEM((key_count, 2 * HD), BF16),
        pltpu.SemaphoreType.DMA((2,)),
        pltpu.SemaphoreType.DMA((2,)),
        pltpu.SemaphoreType.DMA((8, kv_count)),
        pltpu.SemaphoreType.DMA((8, kv_count)),
    ]
    return pl.pallas_call(
        functools.partial(kernel, kv_count, tp_count),
        out_shape=(
            jax.ShapeDtypeStruct((share, out_width), BF16),
            jax.ShapeDtypeStruct((step_rows.shape[0], out_width), BF16),
        ),
        in_specs=[vmem] * 6 + [anywhere] * 2 + [smem] * 3 + [vmem] * 2,
        out_specs=(vmem, vmem),
        scratch_shapes=scratch,
        compiler_params=pltpu.CompilerParams(
            collective_id=0, has_side_effects=True, vmem_limit_bytes=48 * 1024 * 1024
        ),
    )(
        prompt_rows,
        step_rows,
        norm_gain.reshape(1, -1),
        w_query,
        w_key,
        w_value,
        w_output,
        kv_cache,
        step_lengths,
        rollout_ids,
        resume_offsets,
        stretch_rollout.reshape(-1, HD),
        inverse,
    )


def solution(mesh):
    in_specs = (
        P("groups", "kv"),
        P("groups", "kv"),
        P("kv"),
        P("kv", "tp"),
        P("kv", "tp"),
        P("kv", "tp"),
        P("tp", "kv"),
        P("groups", "kv", "tp"),
        P("groups"),
        P("groups"),
        P("groups"),
        P("groups"),
    )
    out_specs = (P(("groups", "tp"), "kv"), P("groups", "kv"))
    return jax.shard_map(
        on_device, mesh=mesh, in_specs=in_specs, out_specs=out_specs, check_vma=False
    )
```

time: 457 us -> 200 us (0.44)
  waiting for transfers between devices: 225 us -> 0 us
  Pallas kernels: 0 us -> 186 us
  blocking collectives: 77.8 us -> 0 us
  starting transfers between devices: 75.5 us -> 0 us
  other arithmetic: 19.4 us -> 0 us
  matrix products: 17.1 us -> 0 us
  between operations: 17.7 us -> 0.67 us
  local copies, waits for them, and re-layouts: 22.2 us -> 12.5 us
    pallas_call x0 -> x1, Pallas kernels: none -> 186 us  [on_device(): pl.pallas_call(functools.partial(kernel, kv_count, tp_count), out_shape=(...]
    all_to_all x4 -> x0, waiting for transfers between devices: 134 us -> none  [the longest x2 117 us: sent_and_summed(): lax.all_to_all(split_up(value, dim, devices), axis, 0, 0, tiled=True)]
    psum x1 -> x0, waiting for transfers between devices: 90.8 us -> none  [on_device(): lax.psum((prompt_state[1] * prompt_factor, prompt_state[2] * prompt_facto...]
    psum x1 -> x0, blocking collectives: 46.8 us -> none  [on_device(): lax.psum((prompt_state[1] * prompt_factor, prompt_state[2] * prompt_facto...]
    ppermute x2 -> x0, starting transfers between devices: 45.5 us -> none  [swapped(): return lax.ppermute(block, axis, route)]
    all_gather x1 -> x0, blocking collectives: 31 us -> none  [side_by_side(): filled, at, outs = (lax.all_gather(both, axis, axis=dim, tiled=True), 0, [])]
    all_to_all x4 -> x0, starting transfers between devices: 29.8 us -> none  [the longest x2 21.2 us: sent_to_all(): return lax.all_to_all(copies, axis, split_axis=0, concat_axis=0, tiled=True)]
    dot_general x12 -> x0, matrix products: 17.1 us -> none  [the longest x4 6.21 us: absorb(): jnp.einsum(form, weights.astype(jnp.bfloat16), values, preferred_element_...]
  transfers between devices with their start and end apart: 7 -> 0, of which waited for: 5 -> 0; matrix products, arithmetic and copies ran while one was open for 3% -> 0% of each run, Pallas kernels for 0% -> 0%
where the time goes in v1:
time: 200 us; the launch traced here: 199 us
  Pallas kernels  186 us (93%)
  local copies, waits for them, and re-layouts  12.5 us (6%)
    pallas_call x1, Pallas kernels, on_device(): pl.pallas_call(functools.partial(kernel, kv_count, tp_count), out_shape=(...  186 us
    unnamed x24, local copies, waits for them, and re-layouts  11.8 us

profile of v1, /device:TPU:65, one launch (start us, length us, event | category | flops | bytes accessed | tf_op | source)
XLA Modules:
  0.0 199.3 jit_solution(15392167360225098649)
XLA Ops:
  0.6 0.7 reshape.10.gain_ref
  1.3 1.0 copy.15.wk_ref
  2.3 1.0 copy.16.wv_ref
  3.2 0.0 copy-start
  3.3 1.6 copy-done
  4.8 0.0 copy-start.1
  4.8 1.0 copy-done.1
  5.9 0.0 copy-start.2
  5.9 1.0 copy-done.2
  6.9 0.0 copy-start.3
  6.9 1.0 copy-done.3
  8.0 0.0 copy-start.4
  8.0 0.7 copy-done.4
  8.6 0.0 copy-start.5
  8.6 0.7 copy-done.5
  9.3 0.0 copy-start.6
  9.3 0.7 copy-done.6
  10.0 0.0 copy-start.7
  10.0 0.7 copy-done.7
  10.6 0.0 copy-start.8
  10.6 0.7 copy-done.8
  11.3 0.0 copy-start.9
  11.3 0.7 copy-done.9
  12.0 186.2 %shard_map.140 = (bf16[32,512]{1,0:T(8,128)(2,1)S(1)}, bf16[2,512]{1,0:T(2,128)(2,1)S(1)}) custom-call(bf16[512,512]{1,0:T(8,128)(2,1)S(1)} %copy-done.1, bf16[2,512]{1,0:T(2,128)(2,1)S(1)} %copy-done.4, bf16[1,512]{1,0:T(2,128)(2,1)S(1)} %reshape.10.gain_ref, bf16[512,512]{1,0:T(8,128)(2,1)S(1)} %copy-done.2, bf16[512,64]{1,0:T(8,128)(2,1)S(1)} %copy.15.wk_ref, ...), custom_call_target="tpu_custom_call" | custom-call | tf_op jit(solution)/shard_map/pallas_call | solution.py:508
  198.1 0.6 copy.19
  198.7 0.6 copy.20
Async XLA Ops:
  3.2 1.6 copy-start
  4.8 1.0 copy-start.1
  5.9 1.0 copy-start.2
  6.9 1.0 copy-start.3
  8.0 0.7 copy-start.4
  8.6 0.7 copy-start.5
  9.3 0.7 copy-start.6
  10.0 0.7 copy-start.7
  10.6 0.7 copy-start.8
  11.3 0.7 copy-start.9

commit v2 on v1

--- a/solution.py
+++ b/solution.py
@@ -109,23 +109,33 @@
 def kernel(
     kv_count,
     tp_count,
+    rows_hbm,
+    step_hbm,
+    gain_hbm,
+    wq_hbm,
+    wk_hbm,
+    wv_hbm,
+    wo_hbm,
+    cache_hbm,
+    lengths_hbm,
+    ids_hbm,
+    offsets_hbm,
+    rollout_hbm,
+    inverse_hbm,
+    out_ref,
+    step_out_ref,
     rows_ref,
     step_ref,
     gain_ref,
     wq_ref,
-    wk_ref,
-    wv_ref,
-    wo_hbm,
-    cache_hbm,
+    wkv_ref,
+    wo_ref,
+    cache_ref,
     lengths_ref,
     ids_ref,
     offsets_ref,
     rollout_ref,
     inverse_ref,
-    out_ref,
-    step_out_ref,
-    wo_ref,
-    cache_ref,
     a_send,
     a_recv,
     aux_recv,
@@ -144,6 +154,7 @@
     step_keys_ref,
     step_values_ref,
     local_sem,
+    known_sem,
     pair_sem,
     send_sem,
     recv_sem,
@@ -159,27 +170,59 @@
     total_features = features * kv_count
     partner = tp + 1 - 2 * lax.rem(tp, 2)
 
-    wo_copy = pltpu.make_async_copy(wo_hbm, wo_ref, local_sem.at[0])
-    cache_copy = pltpu.make_async_copy(cache_hbm, cache_ref, local_sem.at[1])
-    wo_copy.start()
-    cache_copy.start()
-
     barrier = pltpu.get_barrier_semaphore()
-
-    def greet(axis, count, here):
-        def one(j, carry):
-            pl.semaphore_signal(
-                barrier,
-                inc=1,
-                device_id={axis: far_first(here, count, j)},
-                device_id_type=MESH,
+    turn = jnp.where(tp == 0, 1, 0)
+    rank = lax.rem(me - turn + kv_count, kv_count)
+    of_rank = lambda k: lax.rem(k + turn, kv_count)
+
+    def enter(axis, peer):
+        pl.semaphore_signal(barrier, inc=1, device_id={axis: peer}, device_id_type=MESH)
+
+    def greet_above(k, carry):
+        enter("kv", of_rank(k))
+        return carry
+
+    lax.fori_loop(rank + 1, kv_count, greet_above, 0)
+
+    def greet_tp(j, carry):
+        enter("tp", far_first(tp, tp_count, j))
+        return carry
+
+    lax.fori_loop(0, tp_count - 1, greet_tp, 0)
+
+    half = wk_hbm.shape[0]
+    loads = [
+        pltpu.make_async_copy(source, target, local_sem.at[k])
+        for k, (source, target) in enumerate(
+            (
+                (rows_hbm, rows_ref),
+                (wq_hbm, wq_ref),
+                (wk_hbm, wkv_ref.at[:half]),
+                (wv_hbm, wkv_ref.at[half:]),
+                (gain_hbm, gain_ref),
+                (step_hbm, step_ref),
+                (cache_hbm, cache_ref),
+                (wo_hbm, wo_ref),
+                (lengths_hbm, lengths_ref),
+                (ids_hbm, ids_ref),
+                (offsets_hbm, offsets_ref),
+                (rollout_hbm, rollout_ref),
+                (inverse_hbm, inverse_ref),
             )
-            return carry
-
-        lax.fori_loop(0, count - 1, one, 0)
-
-    greet("kv", kv_count, me)
-    greet("tp", tp_count, tp)
+        )
+    ]
+    for load in loads:
+        load.start()
+
+    pl.semaphore_wait(barrier, rank + tp_count - 1)
+
+    def greet_below(k, carry):
+        pl.semaphore_signal(
+            known_sem.at[me], inc=1, device_id={"kv": of_rank(k)}, device_id_type=MESH
+        )
+        return carry
+
+    lax.fori_loop(0, rank, greet_below, 0)
 
     def remote(phase, axis, peer, source, slot_ref, slot):
         return pltpu.make_async_remote_copy(
@@ -217,7 +260,9 @@
 
         lax.fori_loop(0, count - 1, one, 0)
 
-    gain = gain_ref[...].astype(F32)
+    for load in loads[:6]:
+        load.wait()
+    gain = gain_ref[...].astype(F32).reshape(1, features)
     wide = rows_ref[...].astype(F32)
     normed = (wide * gain).astype(BF16)
     step_wide = jnp.concatenate(
@@ -230,29 +275,43 @@
         high, low = high_low(value * value)
         return dot_t(ones, high.astype(BF16)) + dot_t(ones, low.astype(BF16))
 
-    weight_pair = jnp.concatenate([wk_ref[...], wv_ref[...]], axis=1)
     square_high, square_low = high_low(
         jnp.concatenate([squares(wide), squares(step_wide)], axis=1)
     )
     step_part = jnp.concatenate(
-        [dot(step_normed, wq_ref[...])[:8], dot(step_normed, weight_pair)[:8]], axis=1
+        [dot(step_normed, wq_ref[...])[:8], dot_t(step_normed, wkv_ref[...])[:8]], axis=1
     )
     aux_row = iota(step_part.shape, 0)
     aux = jnp.where(
         aux_row == SEQS, square_high, jnp.where(aux_row == SEQS + 1, square_low, step_part)
     )
-    aux_recv[me] = aux.astype(BF16)
+    aux_recv[me] = aux[: SEQS + 2].astype(BF16)
     a_send[:, :, :width] = dot(normed, wq_ref[...]).astype(BF16).reshape(kv_count, share, width)
-    a_send[:, :, width:] = dot(normed, weight_pair).astype(BF16).reshape(kv_count, share, HD)
+    a_send[:, :, width:] = dot_t(normed, wkv_ref[...]).astype(BF16).reshape(kv_count, share, HD)
     a_recv[me] = a_send[me]
 
-    pl.semaphore_wait(barrier, kv_count + tp_count - 2)
     aux_source = lambda peer: aux_recv.at[me]
     a_source = lambda peer: a_send.at[peer]
-    to_all(0, "kv", kv_count, me, aux_source, aux_recv)
-    to_all(1, "kv", kv_count, me, a_source, a_recv)
-
-    cache_copy.wait()
+
+    def partials_to(peer):
+        remote(0, "kv", peer, aux_source(peer), aux_recv, me).start()
+        remote(1, "kv", peer, a_source(peer), a_recv, me).start()
+
+    def send_below(k, carry):
+        partials_to(of_rank(k))
+        return carry
+
+    def send_above(k, carry):
+        peer = of_rank(k)
+        pl.semaphore_wait(known_sem.at[peer], 1)
+        partials_to(peer)
+        return carry
+
+    lax.fori_loop(0, rank, send_below, 0)
+    lax.fori_loop(rank + 1, kv_count, send_above, 0)
+
+    for load in loads[6:]:
+        load.wait()
     keys_ref[:block, :HD] = cache_ref[SEQS + ids_ref[0], :, :HD]
     keys_ref[:block, HD:] = cache_ref[SEQS + ids_ref[1], :, :HD]
     values_ref[:block, :HD] = cache_ref[SEQS + ids_ref[0], :, HD:]
@@ -261,10 +320,9 @@
     step_keys_ref[:block, HD:] = cache_ref[1, :, :HD]
     step_values_ref[:block, :HD] = cache_ref[0, :, HD:]
     step_values_ref[:block, HD:] = cache_ref[1, :, HD:]
-    wo_copy.wait()
 
     first_count = jnp.sum(
-        jnp.sum((rollout_ref[...] == 0).astype(F32), axis=1, keepdims=True), axis=0, keepdims=True
+        (rollout_ref[...].reshape(1, row_count) == 0).astype(F32), axis=1, keepdims=True
     )
     offset_0 = offsets_ref[0].astype(F32)
     offset_1 = offsets_ref[1].astype(F32)
@@ -290,7 +348,7 @@
 
     scale = own_scale(me * share, share)
     step_scale = own_scale(row_count, 8)
-    step_raw = aux_sum * step_scale
+    step_raw = jnp.concatenate([aux_sum, jnp.zeros_like(aux_sum)], axis=0) * step_scale
 
     all_arrive(1, "kv", kv_count, me, a_recv)
     raw = a_recv[0].astype(F32)
@@ -351,7 +409,7 @@
     step_mixed = attend(
         step_queries, sequence > 0, step_allowed, step_keys_ref[...], step_values_ref[...]
     )
-    cs_recv[me] = packed(*step_mixed, 8)
+    cs_recv[me] = packed(*step_mixed, 8)[:SEQS]
     cs_source = lambda peer: cs_recv.at[me]
     to_all(3, "kv", kv_count, me, cs_source, cs_recv)
 
@@ -401,8 +459,8 @@
 
     all_arrive(3, "kv", kv_count, me, cs_recv)
     step_mix = combined(cs_recv, kv_count)
-    step_mix = jnp.concatenate([step_mix, jnp.zeros_like(step_mix)], axis=0).astype(BF16)
-    es_recv[tp] = dot(step_mix, wo_ref[...])[:8].astype(BF16)
+    step_mix = jnp.concatenate([step_mix, jnp.zeros((16 - SEQS, width), F32)], axis=0)
+    es_recv[tp] = dot(step_mix.astype(BF16), wo_ref[...])[:SEQS].astype(BF16)
     es_source = lambda peer: es_recv.at[tp]
     to_all(5, "tp", tp_count, tp, es_source, es_recv)
 
@@ -437,7 +495,7 @@
     step_total = es_recv[0].astype(F32)
     for s in range(1, tp_count):
         step_total += es_recv[s].astype(F32)
-    step_out_ref[...] = step_total[:SEQS].astype(BF16)
+    step_out_ref[...] = step_total.astype(BF16)
     all_arrive(7, "tp", tp_count, tp, e_recv)
     total = e_recv[0].astype(F32)
     for s in range(1, tp_count):
@@ -478,29 +536,39 @@
     frequency = np.exp(np.arange(HD // 2) * (-2.0 * math.log(THETA) / HD)).astype(np.float32)
     inverse = jnp.asarray(np.concatenate([frequency, frequency])[None, :])
     vmem = pl.BlockSpec(memory_space=pltpu.VMEM)
-    smem = pl.BlockSpec(memory_space=pltpu.SMEM)
     anywhere = pl.BlockSpec(memory_space=pl.ANY)
     scratch = [
+        pltpu.VMEM(prompt_rows.shape, BF16),
+        pltpu.VMEM(step_rows.shape, BF16),
+        pltpu.VMEM(norm_gain.shape, BF16),
+        pltpu.VMEM(w_query.shape, BF16),
+        pltpu.VMEM((HD, features), BF16),
         pltpu.VMEM(w_output.shape, BF16),
         pltpu.VMEM(kv_cache.shape, BF16),
+        pltpu.SMEM(step_lengths.shape, jnp.int32),
+        pltpu.SMEM(rollout_ids.shape, jnp.int32),
+        pltpu.SMEM(resume_offsets.shape, jnp.int32),
+        pltpu.VMEM(stretch_rollout.shape, jnp.int32),
+        pltpu.VMEM((1, HD), F32),
         pltpu.VMEM((kv_count, share, width + HD), BF16),
         pltpu.VMEM((kv_count, share, width + HD), BF16),
-        pltpu.VMEM((kv_count, 8, width + HD), BF16),
+        pltpu.VMEM((kv_count, SEQS + 2, width + HD), BF16),
         pltpu.VMEM((share + 8, HD), F32),
         pltpu.VMEM((share + 8, HD), F32),
         pltpu.VMEM((kv_count, share, width), BF16),
         pltpu.VMEM((kv_count, share, width + HD), BF16),
         pltpu.VMEM((kv_count, share, width + HD), BF16),
-        pltpu.VMEM((kv_count, 8, width + HD), BF16),
+        pltpu.VMEM((kv_count, SEQS, width + HD), BF16),
         pltpu.VMEM((kv_count, share, width), BF16),
         pltpu.VMEM((tp_count, share, out_width), BF16),
         pltpu.VMEM((tp_count, share, out_width), BF16),
-        pltpu.VMEM((tp_count, 8, out_width), BF16),
+        pltpu.VMEM((tp_count, SEQS, out_width), BF16),
         pltpu.VMEM((key_count, 2 * HD), BF16),
         pltpu.VMEM((key_count, 2 * HD), BF16),
         pltpu.VMEM((key_count, 2 * HD), BF16),
         pltpu.VMEM((key_count, 2 * HD), BF16),
-        pltpu.SemaphoreType.DMA((2,)),
+        pltpu.SemaphoreType.DMA((13,)),
+        pltpu.SemaphoreType.REGULAR((kv_count,)),
         pltpu.SemaphoreType.DMA((2,)),
         pltpu.SemaphoreType.DMA((8, kv_count)),
         pltpu.SemaphoreType.DMA((8, kv_count)),
@@ -511,25 +579,25 @@
             jax.ShapeDtypeStruct((share, out_width), BF16),
             jax.ShapeDtypeStruct((step_rows.shape[0], out_width), BF16),
         ),
-        in_specs=[vmem] * 6 + [anywhere] * 2 + [smem] * 3 + [vmem] * 2,
+        in_specs=[anywhere] * 13,
         out_specs=(vmem, vmem),
         scratch_shapes=scratch,
         compiler_params=pltpu.CompilerParams(
-            collective_id=0, has_side_effects=True, vmem_limit_bytes=48 * 1024 * 1024
+            collective_id=0, has_side_effects=True, vmem_limit_bytes=62 * 1024 * 1024
         ),
     )(
         prompt_rows,
         step_rows,
-        norm_gain.reshape(1, -1),
+        norm_gain,
         w_query,
-        w_key,
-        w_value,
+        w_key.T,
+        w_value.T,
         w_output,
         kv_cache,
         step_lengths,
         rollout_ids,
         resume_offsets,
-        stretch_rollout.reshape(-1, HD),
+        stretch_rollout,
         inverse,
     )
 

time: 200 us -> 187 us (0.935)
  local copies, waits for them, and re-layouts: 12.5 us -> 2.62 us
  Pallas kernels: 186 us -> 183 us
    unnamed x24 -> x2, local copies, waits for them, and re-layouts: 11.8 us -> 2.62 us
    pallas_call x1, Pallas kernels: 186 us -> 183 us  [on_device(): pl.pallas_call(functools.partial(kernel, kv_count, tp_count), out_shape=(...]
where the time goes in v2:
time: 187 us
  Pallas kernels  183 us (98%)
  local copies, waits for them, and re-layouts  2.62 us (1%)
    pallas_call x1, Pallas kernels, on_device(): pl.pallas_call(functools.partial(kernel, kv_count, tp_count), out_shape=(...  183 us

profile of v2, /device:TPU:65, one launch (start us, length us, event | category | flops | bytes accessed | tf_op | source)
XLA Modules:
  0.0 186.5 jit_solution(6943390377144621773)
XLA Ops:
  0.6 183.3 %shard_map.140 = (bf16[32,512]{1,0:T(8,128)(2,1)}, bf16[2,512]{1,0:T(2,128)(2,1)}) custom-call(bf16[512,512]{1,0:T(8,128)(2,1)} %rows_hbm.1, bf16[2,512]{1,0:T(2,128)(2,1)} %step_hbm.1, bf16[512]{0:T(512)(128)(2,1)} %gain_hbm.1, bf16[512,512]{1,0:T(8,128)(2,1)} %wq_hbm.1, bf16[64,512]{1,0:T(8,128)(2,1)} %bitcast.2, bf16[64,512]{1,0:T(8,128)(2,1)} %bitcast.3, ...), custom_call_target="tpu_custom_call" | custom-call | tf_op jit(solution)/shard_map/pallas_call | solution.py:576
  183.9 1.4 copy.17
  185.3 1.2 copy.18
